TPU v7x, 32 devices: a whole 2x2x4 slice. The times are simulated.
32 devices in a mesh: clip: 16 (over z, x, core), seq: 2 (over y).
Axes of the slice: x: 2, y: 2, z: 4, core: 2. Of those that a mesh axis runs over, the one named last changes fastest.
Arguments:
- frames: bfloat16 [16, 1500, 768], P('clip', 'seq'), may hold values from -6 to 6
- norm1_gain: bfloat16 [768], P(('clip', 'seq')), may hold values from 0.5 to 1.5
- norm1_shift: bfloat16 [768], P(('clip', 'seq')), may hold values from -3 to 3
- query_weight: bfloat16 [768, 768], P(('clip', 'seq')), may hold values from -0.21875 to 0.21875
- query_bias: bfloat16 [768], P(('clip', 'seq')), may hold values from -3 to 3
- key_weight: bfloat16 [768, 768], P(('clip', 'seq')), may hold values from -0.21875 to 0.21875
- value_weight: bfloat16 [768, 768], P(('clip', 'seq')), may hold values from -0.21875 to 0.21875
- value_bias: bfloat16 [768], P(('clip', 'seq')), may hold values from -3 to 3
- out_weight: bfloat16 [768, 768], P(('clip', 'seq')), may hold values from -6 to 6
- out_bias: bfloat16 [768], P(('clip', 'seq')), may hold values from -3 to 3
- norm2_gain: bfloat16 [768], P(('clip', 'seq')), may hold values from 0.5 to 1.5
- norm2_shift: bfloat16 [768], P(('clip', 'seq')), may hold values from -3 to 3
- hidden_weight: bfloat16 [768, 3072], P(('clip', 'seq')), may hold values from -0.21875 to 0.21875
- hidden_bias: bfloat16 [3072], P(('clip', 'seq')), may hold values from -3 to 3
- output_weight: bfloat16 [3072, 768], P(('clip', 'seq')), may hold values from -0.109375 to 0.109375
- output_bias: bfloat16 [768], P(('clip', 'seq')), may hold values from -3 to 3
- out_grad: bfloat16 [16, 1500, 768], P('clip', 'seq'), may hold values from -6 to 6
Outputs:
- encoded: bfloat16 [16, 1500, 768], P('clip', 'seq')
- frames_grad: bfloat16 [16, 1500, 768], P('clip', 'seq')
- norm1_gain_grad: float32 [768], P(('clip', 'seq'))
- norm1_shift_grad: float32 [768], P(('clip', 'seq'))
- query_weight_grad: float32 [768, 768], P(('clip', 'seq'))
- query_bias_grad: float32 [768], P(('clip', 'seq'))
- key_weight_grad: float32 [768, 768], P(('clip', 'seq'))
- value_weight_grad: float32 [768, 768], P(('clip', 'seq'))
- value_bias_grad: float32 [768], P(('clip', 'seq'))
- out_weight_grad: float32 [768, 768], P(('clip', 'seq'))
- out_bias_grad: float32 [768], P(('clip', 'seq'))
- norm2_gain_grad: float32 [768], P(('clip', 'seq'))
- norm2_shift_grad: float32 [768], P(('clip', 'seq'))
- hidden_weight_grad: float32 [768, 3072], P(('clip', 'seq'))
- hidden_bias_grad: float32 [3072], P(('clip', 'seq'))
- output_weight_grad: float32 [3072, 768], P(('clip', 'seq'))
- output_bias_grad: float32 [768], P(('clip', 'seq'))
All inputs are finite; a program needn't handle non-finite values.
Results may differ from a plain program's by a relative error of at most 0.012.
Values may be sent and summed in bfloat16 or wider, within the bound.
A program may use at most 256 MiB of HBM per device.

v0:
```python
import jax
import jax.numpy as jnp
from jax import lax
from jax.sharding import PartitionSpec as P

HD = 64


epsilon = 1e-05
heads_together = 4


def layer_norm(rows_in, gain_vec, shift_vec):
    center = rows_in - jnp.mean(rows_in, axis=-1, keepdims=True)
    spread = jnp.mean(center * center, axis=-1, keepdims=True)
    return center * lax.rsqrt(spread + epsilon) * gain_vec + shift_vec


def gelu_exact(rows_in):
    return 0.5 * rows_in * (1.0 + lax.erf(rows_in * 0.7071067811865476))


def matmul(left, right):
    return jnp.dot(left, right, preferred_element_type=jnp.float32)


def left_matmul(left, right):
    return lax.dot_general(
        left, right, (((0,), (0,)), ((), ())), preferred_element_type=jnp.float32
    )


def right_matmul(left, right):
    return lax.dot_general(
        left, right, (((1,), (1,)), ((), ())), preferred_element_type=jnp.float32
    )


def head_groups(rows_in):
    row_count = rows_in.shape[0]
    group_count = rows_in.shape[1] // (heads_together * HD)
    return rows_in.reshape(row_count, group_count, heads_together, HD).transpose(1, 2, 0, 3)


def merge_groups(grouped):
    return grouped.transpose(2, 0, 1, 3).reshape(grouped.shape[2], -1)


def attend_clip(operands):
    query_clip, key_clip, value_clip = operands

    def attend_group(group_in):
        query_grp, key_grp, value_grp = group_in
        scores = jnp.einsum(
            "hqd,hkd->hqk", query_grp, key_grp, preferred_element_type=jnp.float32
        ) * HD ** (-0.5)
        row_max = jnp.max(scores, axis=-1, keepdims=True)
        exp_scores = jnp.exp(scores - row_max)
        row_total = jnp.sum(exp_scores, axis=-1, keepdims=True)
        soft_probs = (exp_scores / row_total).astype(jnp.bfloat16)
        attended = jnp.einsum(
            "hqk,hkd->hqd", soft_probs, value_grp, preferred_element_type=jnp.float32
        )
        return (attended, row_max[..., 0] + jnp.log(row_total[..., 0]))

    attended, log_total = lax.map(
        attend_group, (head_groups(query_clip), head_groups(key_clip), head_groups(value_clip))
    )
    return (merge_groups(attended), log_total)


def attend_back(operands):
    query_clip, key_clip, value_clip, grad_clip, log_total = operands

    def back_group(group_in):
        query_grp, key_grp, value_grp, grad_grp, log_grp = group_in
        scores = jnp.einsum(
            "hqd,hkd->hqk", query_grp, key_grp, preferred_element_type=jnp.float32
        ) * HD ** (-0.5)
        soft_probs = jnp.exp(scores - log_grp[..., None])
        value_grad = jnp.einsum(
            "hqk,hqd->hkd",
            soft_probs.astype(jnp.bfloat16),
            grad_grp,
            preferred_element_type=jnp.float32,
        )
        prob_grad = jnp.einsum(
            "hqd,hkd->hqk", grad_grp, value_grp, preferred_element_type=jnp.float32
        )
        row_inner = jnp.sum(soft_probs * prob_grad, axis=-1, keepdims=True)
        score_grad = (soft_probs * (prob_grad - row_inner)).astype(jnp.bfloat16)
        query_grad = jnp.einsum(
            "hqk,hkd->hqd", score_grad, key_grp, preferred_element_type=jnp.float32
        ) * HD ** (-0.5)
        key_grad = jnp.einsum(
            "hqk,hqd->hkd", score_grad, query_grp, preferred_element_type=jnp.float32
        ) * HD ** (-0.5)
        return (query_grad, key_grad, value_grad)

    query_grad, key_grad, value_grad = lax.map(
        back_group,
        (
            head_groups(query_clip),
            head_groups(key_clip),
            head_groups(value_clip),
            head_groups(grad_clip),
            log_total,
        ),
    )
    return (merge_groups(query_grad), merge_groups(key_grad), merge_groups(value_grad))


def column_sums(rows_in):
    return jnp.sum(rows_in.astype(jnp.float32), axis=0)


def per_device(
    frames,
    norm1_gain,
    norm1_shift,
    query_weight,
    query_bias,
    key_weight,
    value_weight,
    value_bias,
    out_weight,
    out_bias,
    norm2_gain,
    norm2_shift,
    hidden_weight,
    hidden_bias,
    output_weight,
    output_bias,
    out_grad,
):
    (
        gain_one,
        shift_one,
        w_query,
        b_query,
        w_key,
        w_value,
        b_value,
        w_out,
        b_out,
        gain_two,
        shift_two,
        w_hidden,
        b_hidden,
        w_output,
        b_output,
    ) = (
        lax.all_gather(norm1_gain, ("clip", "seq"), axis=0, tiled=True),
        lax.all_gather(norm1_shift, ("clip", "seq"), axis=0, tiled=True),
        lax.all_gather(query_weight, ("clip", "seq"), axis=0, tiled=True),
        lax.all_gather(query_bias, ("clip", "seq"), axis=0, tiled=True),
        lax.all_gather(key_weight, ("clip", "seq"), axis=0, tiled=True),
        lax.all_gather(value_weight, ("clip", "seq"), axis=0, tiled=True),
        lax.all_gather(value_bias, ("clip", "seq"), axis=0, tiled=True),
        lax.all_gather(out_weight, ("clip", "seq"), axis=0, tiled=True),
        lax.all_gather(out_bias, ("clip", "seq"), axis=0, tiled=True),
        lax.all_gather(norm2_gain, ("clip", "seq"), axis=0, tiled=True),
        lax.all_gather(norm2_shift, ("clip", "seq"), axis=0, tiled=True),
        lax.all_gather(hidden_weight, ("clip", "seq"), axis=0, tiled=True),
        lax.all_gather(hidden_bias, ("clip", "seq"), axis=0, tiled=True),
        lax.all_gather(output_weight, ("clip", "seq"), axis=0, tiled=True),
        lax.all_gather(output_bias, ("clip", "seq"), axis=0, tiled=True),
    )
    clip_count, frame_rows, model_width = frames.shape
    total_rows = clip_count * frame_rows
    inputs = frames.astype(jnp.float32).reshape(total_rows, model_width)
    normed_full, norm_one_pull = jax.vjp(
        layer_norm, inputs, gain_one.astype(jnp.float32), shift_one.astype(jnp.float32)
    )
    normed = normed_full.astype(jnp.bfloat16)
    query_rows = (matmul(normed, w_query) + b_query).astype(jnp.bfloat16)
    key_rows = matmul(normed, w_key).astype(jnp.bfloat16)
    value_rows = (matmul(normed, w_value) + b_value).astype(jnp.bfloat16)
    key_all, value_all = (
        lax.all_gather(
            key_rows.reshape(clip_count, frame_rows, model_width), "seq", axis=1, tiled=True
        ),
        lax.all_gather(
            value_rows.reshape(clip_count, frame_rows, model_width), "seq", axis=1, tiled=True
        ),
    )
    query_clips = query_rows.reshape(clip_count, frame_rows, model_width)
    attended, log_total = lax.map(attend_clip, (query_clips, key_all, value_all))
    attended = attended.reshape(total_rows, model_width).astype(jnp.bfloat16)
    hidden_in = inputs + matmul(attended, w_out) + b_out
    normed_two_full, norm_two_pull = jax.vjp(
        layer_norm, hidden_in, gain_two.astype(jnp.float32), shift_two.astype(jnp.float32)
    )
    normed_two = normed_two_full.astype(jnp.bfloat16)
    pre_act = matmul(normed_two, w_hidden) + b_hidden
    acted_full, gelu_pull = jax.vjp(gelu_exact, pre_act)
    acted = acted_full.astype(jnp.bfloat16)
    result = (
        (hidden_in + matmul(acted, w_output) + b_output).astype(jnp.bfloat16).reshape(frames.shape)
    )
    weights_back = (
        lax.all_gather(norm1_gain, ("clip", "seq"), axis=0, tiled=True),
        lax.all_gather(norm1_shift, ("clip", "seq"), axis=0, tiled=True),
        lax.all_gather(query_weight, ("clip", "seq"), axis=0, tiled=True),
        lax.all_gather(query_bias, ("clip", "seq"), axis=0, tiled=True),
        lax.all_gather(key_weight, ("clip", "seq"), axis=0, tiled=True),
        lax.all_gather(value_weight, ("clip", "seq"), axis=0, tiled=True),
        lax.all_gather(value_bias, ("clip", "seq"), axis=0, tiled=True),
        lax.all_gather(out_weight, ("clip", "seq"), axis=0, tiled=True),
        lax.all_gather(out_bias, ("clip", "seq"), axis=0, tiled=True),
        lax.all_gather(norm2_gain, ("clip", "seq"), axis=0, tiled=True),
        lax.all_gather(norm2_shift, ("clip", "seq"), axis=0, tiled=True),
        lax.all_gather(hidden_weight, ("clip", "seq"), axis=0, tiled=True),
        lax.all_gather(hidden_bias, ("clip", "seq"), axis=0, tiled=True),
        lax.all_gather(output_weight, ("clip", "seq"), axis=0, tiled=True),
        lax.all_gather(output_bias, ("clip", "seq"), axis=0, tiled=True),
    )
    (
        gain_one,
        shift_one,
        w_query,
        b_query,
        w_key,
        w_value,
        b_value,
        w_out,
        b_out,
        gain_two,
        shift_two,
        w_hidden,
        b_hidden,
        w_output,
        b_output,
    ) = weights_back
    grad_out = out_grad.astype(jnp.float32).reshape(total_rows, model_width)
    grad_ff = grad_out.astype(jnp.bfloat16)
    grad_w_output = left_matmul(acted, grad_ff)
    grad_b_output = column_sums(grad_ff)
    grad_pre = gelu_pull(right_matmul(grad_ff, w_output))[0].astype(jnp.bfloat16)
    grad_w_hidden = left_matmul(normed_two, grad_pre)
    grad_b_hidden = column_sums(grad_pre)
    grad_from_norm, grad_gain_two, grad_shift_two = norm_two_pull(right_matmul(grad_pre, w_hidden))
    grad_hidden_in = grad_out + grad_from_norm
    grad_branch = grad_hidden_in.astype(jnp.bfloat16)
    grad_w_out = left_matmul(attended, grad_branch)
    grad_b_out = column_sums(grad_branch)
    grad_attended = right_matmul(grad_branch, w_out).astype(jnp.bfloat16)
    query_grad, key_grad, value_grad = lax.map(
        attend_back,
        (
            query_clips,
            key_all,
            value_all,
            grad_attended.reshape(clip_count, frame_rows, model_width),
            log_total,
        ),
    )
    key_grad, value_grad = (
        lax.psum_scatter(
            key_grad.astype(jnp.bfloat16), "seq", scatter_dimension=1, tiled=True
        ).astype(jnp.float32),
        lax.psum_scatter(
            value_grad.astype(jnp.bfloat16), "seq", scatter_dimension=1, tiled=True
        ).astype(jnp.float32),
    )
    query_grad = query_grad.reshape(total_rows, model_width).astype(jnp.bfloat16)
    key_grad = key_grad.reshape(total_rows, model_width).astype(jnp.bfloat16)
    value_grad = value_grad.reshape(total_rows, model_width).astype(jnp.bfloat16)
    grad_w_query = left_matmul(normed, query_grad)
    grad_b_query = column_sums(query_grad)
    grad_w_key = left_matmul(normed, key_grad)
    grad_w_value = left_matmul(normed, value_grad)
    grad_b_value = column_sums(value_grad)
    grad_normed = (
        right_matmul(query_grad, w_query)
        + right_matmul(key_grad, w_key)
        + right_matmul(value_grad, w_value)
    )
    grad_inputs, grad_gain_one, grad_shift_one = norm_one_pull(grad_normed)
    grad_frames = (grad_inputs + grad_hidden_in).astype(jnp.bfloat16).reshape(frames.shape)
    (
        owned_gain_one,
        owned_shift_one,
        owned_w_query,
        owned_b_query,
        owned_w_key,
        owned_w_value,
        owned_b_value,
        owned_w_out,
        owned_b_out,
        owned_gain_two,
        owned_shift_two,
        owned_w_hidden,
        owned_b_hidden,
        owned_w_output,
        owned_b_output,
    ) = (
        lax.psum_scatter(grad_gain_one, ("clip", "seq"), scatter_dimension=0, tiled=True),
        lax.psum_scatter(grad_shift_one, ("clip", "seq"), scatter_dimension=0, tiled=True),
        lax.psum_scatter(grad_w_query, ("clip", "seq"), scatter_dimension=0, tiled=True),
        lax.psum_scatter(grad_b_query, ("clip", "seq"), scatter_dimension=0, tiled=True),
        lax.psum_scatter(grad_w_key, ("clip", "seq"), scatter_dimension=0, tiled=True),
        lax.psum_scatter(grad_w_value, ("clip", "seq"), scatter_dimension=0, tiled=True),
        lax.psum_scatter(grad_b_value, ("clip", "seq"), scatter_dimension=0, tiled=True),
        lax.psum_scatter(grad_w_out, ("clip", "seq"), scatter_dimension=0, tiled=True),
        lax.psum_scatter(grad_b_out, ("clip", "seq"), scatter_dimension=0, tiled=True),
        lax.psum_scatter(grad_gain_two, ("clip", "seq"), scatter_dimension=0, tiled=True),
        lax.psum_scatter(grad_shift_two, ("clip", "seq"), scatter_dimension=0, tiled=True),
        lax.psum_scatter(grad_w_hidden, ("clip", "seq"), scatter_dimension=0, tiled=True),
        lax.psum_scatter(grad_b_hidden, ("clip", "seq"), scatter_dimension=0, tiled=True),
        lax.psum_scatter(grad_w_output, ("clip", "seq"), scatter_dimension=0, tiled=True),
        lax.psum_scatter(grad_b_output, ("clip", "seq"), scatter_dimension=0, tiled=True),
    )
    return (
        result,
        grad_frames,
        owned_gain_one,
        owned_shift_one,
        owned_w_query,
        owned_b_query,
        owned_w_key,
        owned_w_value,
        owned_b_value,
        owned_w_out,
        owned_b_out,
        owned_gain_two,
        owned_shift_two,
        owned_w_hidden,
        owned_b_hidden,
        owned_w_output,
        owned_b_output,
    )


def solution(mesh):
    placed = (
        P("clip", "seq", None),
        P(("clip", "seq")),
        P(("clip", "seq")),
        P(("clip", "seq"), None),
        P(("clip", "seq")),
        P(("clip", "seq"), None),
        P(("clip", "seq"), None),
        P(("clip", "seq")),
        P(("clip", "seq"), None),
        P(("clip", "seq")),
        P(("clip", "seq")),
        P(("clip", "seq")),
        P(("clip", "seq"), None),
        P(("clip", "seq")),
        P(("clip", "seq"), None),
        P(("clip", "seq")),
        P("clip", "seq", None),
    )
    return jax.shard_map(
        per_device,
        mesh=mesh,
        in_specs=placed,
        out_specs=(
            P("clip", "seq", None),
            P("clip", "seq", None),
            P(("clip", "seq")),
            P(("clip", "seq")),
            P(("clip", "seq"), None),
            P(("clip", "seq")),
            P(("clip", "seq"), None),
            P(("clip", "seq"), None),
            P(("clip", "seq")),
            P(("clip", "seq"), None),
            P(("clip", "seq")),
            P(("clip", "seq")),
            P(("clip", "seq")),
            P(("clip", "seq"), None),
            P(("clip", "seq")),
            P(("clip", "seq"), None),
            P(("clip", "seq")),
        ),
        check_vma=False,
    )
```

profile of v0, /device:TPU:0, one launch (start us, length us, event | category | flops | bytes accessed | tf_op | source)
XLA Modules:
  0.0 1449.7 jit_solution(12208105328299048319)
XLA Ops:
  17.0 42.8 %all-reduce.21 = (bf16[768]{0:T(1024)(128)(2,1)S(1)}, bf16[768]{0:T(1024)(128)(2,1)S(1)}, bf16[768]{0:T(1024)(128)(2,1)S(1)}, bf16[768]{0:T(1024)(128)(2,1)S(1)}...) all-reduce(bf16[768]{0:T(1024)(128)(2,1)S(1)} %dynamic-update-slice, ...), channel_id=1, replica_groups=mesh['clip'=16,'seq'=2] {'clip','seq'}, use_global_device_ids=true, to_apply=%add.2 | all-reduce | flops 9216 | bytes 36864
  71.8 52.1 %all-gather.15.cloned.1.call-done = bf16[768,768]{1,0:T(8,128)(2,1)} async-done(((bf16[24,768]{1,0:T(8,128)(2,1)}), bf16[768,768]{1,0:T(8,128)(2,1)}) %all-gather.15.cloned.1.call-update) | async-done | bytes 1179664 | tf_op jit(solution)/shard_map/all_gather | solution.py:157
  132.2 47.6 %all-gather.13.cloned.1.call-done = bf16[768,768]{1,0:T(8,128)(2,1)} async-done(((bf16[24,768]{1,0:T(8,128)(2,1)}), bf16[768,768]{1,0:T(8,128)(2,1)}) %all-gather.13.cloned.1.call-update) | async-done | bytes 1179664 | tf_op jit(solution)/shard_map/all_gather | solution.py:155
  183.0 33.2 %all-gather.27.cloned.1.call-done = bf16[2,750,768]{2,1,0:T(8,128)(2,1)} async-done(((bf16[1,750,768]{2,1,0:T(8,128)(2,1)}), bf16[2,750,768]{2,1,0:T(8,128)(2,1)}) %all-gather.27.cloned.1.call-update) | async-done | bytes 2304016 | tf_op jit(solution)/shard_map/all_gather | solution.py:183
  225.3 28.3 %all-gather.25.cloned.1.call-done = bf16[2,750,768]{2,1,0:T(8,128)(2,1)} async-done(((bf16[1,750,768]{2,1,0:T(8,128)(2,1)}), bf16[2,750,768]{2,1,0:T(8,128)(2,1)}) %all-gather.25.cloned.1.call-update) | async-done | bytes 2304016 | tf_op jit(solution)/shard_map/all_gather | solution.py:180
  267.3 89.8 %while.46 = (s32[]{:T(128)}, bf16[3,4,750,64]{2,3,1,0:T(8,128)(2,1)}, f32[3,4,750]{2,1,0:T(4,128)}, bf16[3,4,750,64]{2,3,1,0:T(8,128)(2,1)S(1)}, bf16[3,4,1500,6...) while((s32[]{:T(128)}, bf16[3,4,750,64]{2,3,1,0:T(8,128)(2,1)}, ...), condition=%wide.region_5.6_spmd, body=%wide.region_2.5_spmd.sunk | while | flops 1192497024 | bytes 57333164 | solution.py:66
  276.2 10.1 fusion.144
  305.9 10.1 fusion.144
  317.4 9.5 fusion.145
  335.8 10.2 fusion.144
  362.8 13.2 all-gather.21.cloned.1.call-done
  376.0 10.7 multiply_convert_fusion.1
  386.6 54.2 %all-gather.23.cloned.1.call-done = bf16[3072,768]{1,0:T(8,128)(2,1)} async-done(((bf16[96,768]{1,0:T(8,128)(2,1)}), bf16[3072,768]{1,0:T(8,128)(2,1)}) %all-gather.23.cloned.1.call-update) | async-done | bytes 4718608 | tf_op jit(solution)/shard_map/all_gather | solution.py:166
  440.8 11.9 convert_reduce_fusion
  466.6 156.2 %while.47 = (s32[]{:T(128)}, bf16[3,4,750,64]{2,3,1,0:T(8,128)(2,1)}, bf16[3,4,1500,64]{2,3,1,0:T(8,128)(2,1)}, bf16[3,4,1500,64]{2,3,1,0:T(8,128)(2,1)}, bf16[3...) while((s32[]{:T(128)}, ...), condition=%wide.region_12.13_spmd, body=%wide.region_10.12_spmd.sunk | while | flops 2934573056 | bytes 153613056 | solution.py:100
  476.4 12.7 multiply_reduce_fusion.8
  489.1 12.7 multiply_convert_fusion.3
  508.4 10.3 fusion.157
  528.4 12.8 multiply_reduce_fusion.8
  541.1 12.7 multiply_convert_fusion.3
  560.3 10.4 fusion.157
  580.3 12.8 multiply_reduce_fusion.8
  593.1 12.7 multiply_convert_fusion.3
  612.3 10.4 fusion.157
  633.4 107.0 %all-reduce.25.cloned.1.call-done = (bf16[1,1500,768]{1,2,0:T(8,128)(2,1)}, bf16[1,1500,768]{1,2,0:T(8,128)(2,1)}) async-done(((bf16[1,1500,768]{1,2,0:T(8,128)(2,1)}, bf16[1,1500,768]{1,2,0:T(8,128)(2,1)}), (bf16[1,1500,768]{1,2,0:T(8,128)(2,1)}, bf16[1,1500,768]{1,2,0:T(8,128)(2,1)})) %all-reduce.25.cloned.1.call-update) | async-done | bytes 4608016
  761.0 10.2 fusion.73
  793.9 40.3 %all-reduce.20 = (f32[768]{0:T(1024)S(1)}, f32[768]{0:T(1024)S(1)}, f32[768]{0:T(1024)S(1)}, f32[768]{0:T(1024)S(1)}, f32[768]{0:T(1024)S(1)}, /*index=5*/f32[76...) all-reduce(f32[768]{0:T(1024)S(1)} %get-tuple-element.151, ...), channel_id=6, replica_groups=mesh['clip'=16,'seq'=2] {'clip','seq'}, use_global_device_ids=true, to_apply=%region_18.19.clone | all-reduce | flops 9216 | bytes 73728
  846.1 104.5 %reduce-scatter.9.cloned.1.call-done = f32[24,768]{1,0:T(8,128)} async-done(((f32[768,768]{1,0:T(8,128)}), f32[24,768]{1,0:T(8,128)}) %reduce-scatter.9.cloned.1.call-update) | async-done | bytes 73744 | tf_op jit(solution)/shard_map/reduce_scatter | solution.py:300
  950.7 104.4 %reduce-scatter.11.cloned.1.call-done = f32[24,768]{1,0:T(8,128)} async-done(((f32[768,768]{1,0:T(8,128)}), f32[24,768]{1,0:T(8,128)}) %reduce-scatter.11.cloned.1.call-update) | async-done | bytes 73744 | tf_op jit(solution)/shard_map/reduce_scatter | solution.py:302
  1055.0 104.5 %reduce-scatter.13.cloned.1.call-done = f32[24,768]{1,0:T(8,128)} async-done(((f32[768,768]{1,0:T(8,128)}), f32[24,768]{1,0:T(8,128)}) %reduce-scatter.13.cloned.1.call-update) | async-done | bytes 73744 | tf_op jit(solution)/shard_map/reduce_scatter | solution.py:303
  1159.5 141.6 %reduce-scatter.17.cloned.1.call-done = f32[24,3072]{1,0:T(8,128)} async-done(((f32[768,3072]{1,0:T(8,128)}), f32[24,3072]{1,0:T(8,128)}) %reduce-scatter.17.cloned.1.call-update) | async-done | bytes 294928 | tf_op jit(solution)/shard_map/reduce_scatter | solution.py:309
  1301.1 141.5 %reduce-scatter.19.cloned.1.call-done = f32[96,768]{1,0:T(8,128)} async-done(((f32[3072,768]{1,0:T(8,128)}), f32[96,768]{1,0:T(8,128)}) %reduce-scatter.19.cloned.1.call-update) | async-done | bytes 294928 | tf_op jit(solution)/shard_map/reduce_scatter | solution.py:311
  (246 shorter events, 238.0 us)
Async XLA Ops:
  7.2 60.9 %copy-start = (bf16[1,750,768]{2,1,0:T(8,128)(2,1)S(1)}, bf16[1,750,768]{2,1,0:T(8,128)(2,1)}, u32[]{:S(2)}) copy-start(bf16[1,750,768]{2,1,0:T(8,128)(2,1)} %param.21) | copy-start | bytes 3456004
  7.2 60.9 %all-gather.17.cloned.1.call-start = ((), (), s32[]{:S(2)}) async-start(), calls=%async_computation.8 | async-start | bytes 1216512 | tf_op jit(solution)/shard_map/all_gather | solution.py:158
  7.9 115.9 %all-gather.15.cloned.1.call-start = ((), (), s32[]{:S(2)}) async-start(), calls=%async_computation.7 | async-start | bytes 1216512 | tf_op jit(solution)/shard_map/all_gather | solution.py:157
  8.7 171.1 %all-gather.13.cloned.1.call-start = ((), (), s32[]{:S(2)}) async-start(), calls=%async_computation.6 | async-start | bytes 1216512 | tf_op jit(solution)/shard_map/all_gather | solution.py:155
  9.4 206.7 %all-gather.27.cloned.1.call-start = ((), (), s32[]{:S(2)}) async-start(), calls=%async_computation.19 | async-start | bytes 3465216 | tf_op jit(solution)/shard_map/all_gather | solution.py:183
  59.8 119.9 %copy-start.29 = (f32[768]{0:T(1024)}, f32[768]{0:T(1024)S(1)}, u32[]{:S(2)}) copy-start(f32[768]{0:T(1024)S(1)} %convert_element_type.163) | copy-start | bytes 9220
  59.8 119.9 %copy-start.41 = (f32[768]{0:T(1024)}, f32[768]{0:T(1024)S(1)}, u32[]{:S(2)}) copy-start(f32[768]{0:T(1024)S(1)} %convert_element_type.164) | copy-start | bytes 9220
  61.4 118.4 %copy-start.27 = (f32[750]{0:T(1024)}, f32[750]{0:T(1024)S(1)}, u32[]{:S(2)}) copy-start(f32[750]{0:T(1024)S(1)} %broadcast_multiply_fusion.1) | copy-start | bytes 9004
  63.7 116.0 %copy-start.31 = (f32[750]{0:T(1024)}, f32[750]{0:T(1024)S(1)}, u32[]{:S(2)}) copy-start(f32[750]{0:T(1024)S(1)} %fusion.82) | copy-start | bytes 9004
  71.7 181.9 %all-gather.25.cloned.1.call-start = ((), (), s32[]{:S(2)}) async-start(), calls=%async_computation.18 | async-start | bytes 3465216 | tf_op jit(solution)/shard_map/all_gather | solution.py:180
  127.4 229.7 %all-gather.19.cloned.1.call-start = ((), (), s32[]{:S(2)}) async-start(), calls=%async_computation.9 | async-start | bytes 1216512 | tf_op jit(solution)/shard_map/all_gather | solution.py:160
  128.0 248.0 %all-gather.21.cloned.1.call-start = ((), (), s32[]{:S(2)}) async-start(), calls=%async_computation.10 | async-start | bytes 4866048 | tf_op jit(solution)/shard_map/all_gather | solution.py:164
  128.7 312.1 %all-gather.23.cloned.1.call-start = ((), (), s32[]{:S(2)}) async-start(), calls=%async_computation.11 | async-start | bytes 4866048 | tf_op jit(solution)/shard_map/all_gather | solution.py:166
  129.5 611.0 %all-reduce.25.cloned.1.call-start = ((), (), s32[]{:S(2)}) async-start(), calls=%async_computation.20 | async-start | bytes 9437184
  267.3 89.9 %copy-start.43 = (f32[768]{0:T(1024)S(1)}, f32[768]{0:T(1024)}, u32[]{:S(2)}) copy-start(f32[768]{0:T(1024)} %convert_element_type.174) | copy-start | bytes 9220
  360.4 15.6 %copy-start.21 = (f32[768]{0:T(1024)S(1)}, f32[768]{0:T(1024)}, u32[]{:S(2)}) copy-start(f32[768]{0:T(1024)} %convert_element_type.175) | copy-start | bytes 9220
  360.4 15.6 %copy-start.25 = (f32[768]{0:T(1024)S(1)}, f32[768]{0:T(1024)}, u32[]{:S(2)}) copy-start(f32[768]{0:T(1024)} %convert_element_type.176) | copy-start | bytes 9220
  360.4 97.1 %copy-start.19 = (f32[750]{0:T(1024)}, f32[750]{0:T(1024)S(1)}, u32[]{:S(2)}) copy-start(f32[750]{0:T(1024)S(1)} %broadcast_multiply_fusion) | copy-start | bytes 9004
  362.8 94.7 %copy-start.23 = (f32[750]{0:T(1024)}, f32[750]{0:T(1024)S(1)}, u32[]{:S(2)}) copy-start(f32[750]{0:T(1024)S(1)} %fusion.83) | copy-start | bytes 9004
  440.8 12.0 copy-start.5
  440.8 12.0 copy-start.47
  452.8 4.7 copy-start.12
  452.8 4.7 copy-start.38
  622.8 223.4 %reduce-scatter.15.cloned.1.call-start = ((), (), s32[]{:S(2)}) async-start(), calls=%async_computation.15 | async-start | bytes 2433024 | tf_op jit(solution)/shard_map/reduce_scatter | solution.py:305
  626.9 323.8 %reduce-scatter.9.cloned.1.call-start = ((), (), s32[]{:S(2)}) async-start(), calls=%async_computation.12 | async-start | bytes 2433024 | tf_op jit(solution)/shard_map/reduce_scatter | solution.py:300
  631.6 423.5 %reduce-scatter.11.cloned.1.call-start = ((), (), s32[]{:S(2)}) async-start(), calls=%async_computation.13 | async-start | bytes 2433024 | tf_op jit(solution)/shard_map/reduce_scatter | solution.py:302
  745.0 414.5 %reduce-scatter.13.cloned.1.call-start = ((), (), s32[]{:S(2)}) async-start(), calls=%async_computation.14 | async-start | bytes 2433024 | tf_op jit(solution)/shard_map/reduce_scatter | solution.py:303
  750.0 551.1 %reduce-scatter.17.cloned.1.call-start = ((), (), s32[]{:S(2)}) async-start(), calls=%async_computation.16 | async-start | bytes 9732096 | tf_op jit(solution)/shard_map/reduce_scatter | solution.py:309
  760.7 681.9 %reduce-scatter.19.cloned.1.call-start = ((), (), s32[]{:S(2)}) async-start(), calls=%async_computation.17 | async-start | bytes 9732096 | tf_op jit(solution)/shard_map/reduce_scatter | solution.py:311
  776.3 8.8 copy-start.14
  776.4 9.5 copy-start.48
  776.4 9.5 copy-start.49
  (39 other events, 63.6 us)
Sparse Core Ops, SparseCore 0:
  10.9 57.1 all-gather.16
  71.0 52.7 all-gather.14
  126.8 52.9 all-gather.12
  181.7 34.3 all-gather.26
  218.1 35.4 all-gather.24
  256.4 54.0 all-gather.18
  313.4 62.5 all-gather.20
  378.9 61.9 all-gather.22
  622.9 117.5 all-reduce.24
  746.2 99.8 reduce-scatter.14
  852.0 98.6 reduce-scatter.8
  956.4 98.6 reduce-scatter.10
  1060.9 98.6 reduce-scatter.12
  1165.9 135.2 reduce-scatter.16
  1307.4 135.1 reduce-scatter.18
where the time goes:
time: 1460 us; the launch traced here: 1450 us
  waiting for transfers between devices  947 us (65%)
  matrix products  258 us (18%)
  other arithmetic  86 us (6%)
  blocking collectives  83.2 us (6%)
  local copies, waits for them, and re-layouts  58 us (4%)
  between operations  15.6 us (1%)
    reduce_scatter x1, waiting for transfers between devices, per_device(): lax.psum_scatter(grad_w_hidden, ('clip', 'seq'), scatter_dimension=0, til...  142 us
    reduce_scatter x1, waiting for transfers between devices, per_device(): lax.psum_scatter(grad_w_output, ('clip', 'seq'), scatter_dimension=0, til...  142 us
    unnamed x16, waiting for transfers between devices  111 us
    reduce_scatter x1, waiting for transfers between devices, per_device(): lax.psum_scatter(grad_w_query, ('clip', 'seq'), scatter_dimension=0, tile...  105 us
    reduce_scatter x1, waiting for transfers between devices, per_device(): lax.psum_scatter(grad_w_value, ('clip', 'seq'), scatter_dimension=0, tile...  105 us
    reduce_scatter x1, waiting for transfers between devices, per_device(): lax.psum_scatter(grad_w_key, ('clip', 'seq'), scatter_dimension=0, tiled=...  104 us
    unnamed x2, blocking collectives  83.2 us
    all_gather x1, waiting for transfers between devices, per_device(): lax.all_gather(output_weight, ('clip', 'seq'), axis=0, tiled=True)  54.2 us
  transfers between devices with their start and end apart: 15, of which 14 were waited for; matrix products, arithmetic and copies ran while one was open for 14% of the time, Pallas kernels for 0%

commit v1 on v0

v1 whole, which is shorter than its diff:
```python
import functools

import jax
import jax.numpy as jnp
from jax import lax
from jax.experimental import pallas as pl
from jax.experimental.pallas import tpu as pltpu
from jax.sharding import PartitionSpec as P

bf, f32 = jnp.bfloat16, jnp.float32
NEG = -1e30

def nt(a, b):
    return lax.dot_general(a, b, (((1,), (1,)), ((), ())), preferred_element_type=f32)
def nn(a, b):
    return lax.dot_general(a, b, (((1,), (0,)), ((), ())), preferred_element_type=f32)
def tn(a, b):
    return lax.dot_general(a, b, (((0,), (0,)), ((), ())), preferred_element_type=f32)

def lanes(shape):
    return lax.broadcasted_iota(jnp.int32, shape, 1)
def rows(shape):
    return lax.broadcasted_iota(jnp.int32, shape, 0)

def split3(x):
    hi = x.astype(bf); r = x - hi.astype(f32)
    mid = r.astype(bf); lo = (r - mid.astype(f32)).astype(bf)
    return hi.astype(f32), mid.astype(f32), lo.astype(f32)

def fwd_kernel(half, valid, tq, q_ref, k_ref, v_ref, o_ref, wide_ref, l_ref, kc, vc):
    n = k_ref.shape[0]
    @pl.when(pl.program_id(1) == 0)
    def _():
        ln = lanes((n, 128)); pad = lax.rem(rows((n, 128)), half) >= valid
        k = k_ref[...]
        ext = jnp.where((ln == 0) & pad, NEG, 0.0).astype(bf)
        zero = jnp.zeros_like(k)
        kc[0, :, :128] = jnp.where(ln < 64, k, zero)
        kc[1, :, :128] = jnp.where(ln < 64, zero, k)
        kc[0, :, 128:] = ext
        kc[1, :, 128:] = ext
        vc[:, :128] = v_ref[...]
        vc[:, 128:] = jnp.ones((n, 128), bf)
    ln = lanes((tq, 128))
    one = jnp.where(ln == 0, 1.0, 0.0).astype(bf)
    qc = jnp.concatenate([q_ref[...] * jnp.asarray(0.125, bf), one], axis=1)
    outs = []
    for h in range(2):
        s = nt(qc, kc[h])
        m = jnp.max(s, axis=1, keepdims=True)
        p = jnp.exp(s - m).astype(bf)
        o = nn(p, vc[...])
        tot = o[:, 128:]
        outs.append(o[:, :128] / tot)
        l3 = split3(m + jnp.log(tot))
        e = jnp.where(ln == 0, -l3[0], jnp.where(ln == 1, -l3[1], jnp.where(ln == 2, -l3[2], jnp.where(ln == 3, 1.0, 0.0))))
        l_ref[h] = e.astype(bf)
    wide = jnp.where(ln < 64, outs[0], outs[1])
    wide_ref[...] = wide
    o_ref[...] = wide.astype(bf)

def attn_fwd(q, k, v, half, valid, tq=256):
    n, w = q.shape
    np_ = w // 128
    return pl.pallas_call(
        functools.partial(fwd_kernel, half, valid, tq),
        grid=(np_, n // tq),
        out_shape=(jax.ShapeDtypeStruct((n, w), bf), jax.ShapeDtypeStruct((n, w), f32), jax.ShapeDtypeStruct((2 * np_, n, 128), bf)),
        in_specs=[pl.BlockSpec((tq, 128), lambda p, i: (i, p)), pl.BlockSpec((n, 128), lambda p, i: (0, p)), pl.BlockSpec((n, 128), lambda p, i: (0, p))],
        out_specs=[pl.BlockSpec((tq, 128), lambda p, i: (i, p)), pl.BlockSpec((tq, 128), lambda p, i: (i, p)), pl.BlockSpec((2, tq, 128), lambda p, i: (p, i, 0))],
        scratch_shapes=[pltpu.VMEM((2, n, 256), bf), pltpu.VMEM((n, 256), bf)],
        compiler_params=pltpu.CompilerParams(vmem_limit_bytes=60 << 20),
    )(q, k, v)

def bwd_kernel(half, valid, tq, q_ref, k_ref, v_ref, g_ref, o_ref, l_ref, dq_ref, dk_ref, dv_ref, kc, vc, km, dka, dva):
    n = k_ref.shape[0]
    i = pl.program_id(1)
    @pl.when(i == 0)
    def _():
        ln = lanes((n, 128)); pad = lax.rem(rows((n, 128)), half) >= valid
        k = k_ref[...]
        ext = jnp.where(ln < 3, 1.0, jnp.where((ln == 3) & pad, NEG, 0.0)).astype(bf)
        zero = jnp.zeros_like(k)
        kc[:, :128] = k
        kc[:, 128:] = ext
        km[0] = jnp.where(ln < 64, k, zero)
        km[1] = jnp.where(ln < 64, zero, k)
        vc[:, :128] = v_ref[...]
        vc[:, 128:] = ext
        dka[...] = jnp.zeros_like(dka)
        dva[...] = jnp.zeros_like(dva)
    ln = lanes((tq, 128))
    q = q_ref[...] * jnp.asarray(0.125, bf)
    g = g_ref[...]
    go = g.astype(f32) * o_ref[...]
    ps, ds_, qs, gs = [], [], [], []
    dq = jnp.zeros((tq, 128), f32)
    for h in range(2):
        mine = (ln < 64) if h == 0 else (ln >= 64)
        qm = jnp.where(mine, q, jnp.zeros_like(q))
        gm = jnp.where(mine, g, jnp.zeros_like(g))
        d = jnp.sum(jnp.where(mine, go, 0.0), axis=1, keepdims=True)
        d3 = split3(jnp.broadcast_to(d, (tq, 128)))
        de = jnp.where(ln == 0, -d3[0], jnp.where(ln == 1, -d3[1], jnp.where(ln == 2, -d3[2], 0.0))).astype(bf)
        st = nt(kc[...], jnp.concatenate([qm, l_ref[h]], axis=1))
        p = jnp.exp(st)
        dp = nt(vc[...], jnp.concatenate([gm, de], axis=1))
        ds = (p * dp).astype(bf)
        dq = dq + tn(ds, km[h])
        ps.append(p.astype(bf)); ds_.append(ds); qs.append(qm); gs.append(gm)
    dva[...] += nn(ps[0], gs[0]) + nn(ps[1], gs[1])
    dka[...] += nn(ds_[0], qs[0]) + nn(ds_[1], qs[1])
    dq_ref[...] = (dq * 0.125).astype(bf)
    @pl.when(i == pl.num_programs(1) - 1)
    def _():
        dk_ref[...] = dka[...].astype(bf)
        dv_ref[...] = dva[...].astype(bf)

def attn_bwd(q, k, v, g, o, l, half, valid, tq=256):
    n, w = q.shape
    np_ = w // 128
    qs = pl.BlockSpec((tq, 128), lambda p, i: (i, p)); ks = pl.BlockSpec((n, 128), lambda p, i: (0, p))
    return pl.pallas_call(
        functools.partial(bwd_kernel, half, valid, tq),
        grid=(np_, n // tq),
        out_shape=tuple(jax.ShapeDtypeStruct((n, w), bf) for _ in range(3)),
        in_specs=[qs, ks, ks, qs, qs, pl.BlockSpec((2, tq, 128), lambda p, i: (p, i, 0))],
        out_specs=[qs, ks, ks],
        scratch_shapes=[pltpu.VMEM((n, 256), bf), pltpu.VMEM((n, 256), bf), pltpu.VMEM((2, n, 128), bf), pltpu.VMEM((n, 128), f32), pltpu.VMEM((n, 128), f32)],
        compiler_params=pltpu.CompilerParams(vmem_limit_bytes=60 << 20),
    )(q, k, v, g, o, l)
MESH = pl.DeviceIdType.MESH
SEQ = "seq"


class Place:
    def __init__(self, clips):
        self.count = clips.bit_length() - 1
        self.clip = lax.axis_index("clip")
        self.seq = lax.axis_index("seq")
        self.bits = list(reversed(range(self.count))) + [SEQ]

    def mine(self, bit):
        if bit == SEQ:
            return self.seq
        return lax.rem(lax.div(self.clip, 1 << bit), 2)

    def partner(self, bit):
        if bit == SEQ:
            return {"clip": self.clip, "seq": 1 - self.seq}
        return {"clip": self.clip + (1 - 2 * self.mine(bit)) * (1 << bit), "seq": self.seq}

    def index(self, free, flipped=(), without=()):
        out = []
        for bit in self.bits:
            if bit in without:
                continue
            if bit in free:
                out.append(slice(None))
            elif bit in flipped:
                out.append(1 - self.mine(bit))
            else:
                out.append(self.mine(bit))
        return tuple(out)

    def greet(self):
        barrier = pltpu.get_barrier_semaphore()
        for bit in self.bits:
            pl.semaphore_signal(barrier, inc=1, device_id=self.partner(bit), device_id_type=MESH)
        pl.semaphore_wait(barrier, len(self.bits))


def remote(src, dst, sems, partner):
    return pltpu.make_async_remote_copy(
        src_ref=src, dst_ref=dst, send_sem=sems[0], recv_sem=sems[1], device_id=partner, device_id_type=MESH
    )


class Gather:
    def __init__(self, place, shard, out, order, half, sems, local_sem):
        self.place, self.shard, self.out, self.order, self.half = place, shard, out, list(order), half
        self.sems, self.local_sem = sems, local_sem
        self.n_events = len(self.order) + (3 if half is None else 4)
        self.used = 0

    def columns(self, of_seq):
        if self.half is None:
            return self.shard
        return self.shard.at[:, pl.ds(pl.multiple_of(of_seq * self.half, 128), self.half)]

    def copy(self, k, src, dst, bit):
        return remote(src, dst, (self.sems.at[0, k], self.sems.at[1, k]), self.place.partner(bit))

    def local(self):
        return pltpu.make_async_copy(self.columns(self.place.seq), self.out.at[self.place.index(())], self.local_sem)

    def trade(self):
        p = self.place
        return self.copy(0, self.columns(1 - p.seq), self.out.at[p.index(())], SEQ)

    def first_free(self):
        return () if self.half is None else (SEQ,)

    def step(self, k):
        free = self.first_free() + tuple(self.order[:k])
        bit = self.order[k]
        held = self.out.at[self.place.index(free)]
        if k == 0 and self.half is None:
            return self.copy(2 * k + 1, self.shard, held, bit)
        return self.copy(2 * k + 1, held, held, bit)

    def hand(self, k):
        free = self.first_free() + tuple(self.order[:k])
        got = self.out.at[self.place.index(free, flipped=(self.order[k],))]
        return self.copy(2 * k + 2, got, got, 0)

    def hand_own(self):
        own = self.out.at[self.place.index(self.first_free())]
        src = self.shard if self.half is None else own
        return self.copy(2 * len(self.order) + 1, src, own, 0)

    def events(self):
        n = len(self.order)
        run = []
        if self.half is not None:

            def begin():
                self.local().start()
                self.trade().start()

            def first():
                self.local().wait()
                self.trade().wait()
                self.step(0).start()
                self.hand_own().start()

            run += [begin, first]
        else:

            def begin():
                self.local().start()
                self.step(0).start()
                self.hand_own().start()

            run += [begin]
        for k in range(1, n + 1):

            def event(k=k):
                self.step(k - 1).wait_recv()
                if k == 1 and self.half is None:
                    self.local().wait()
                self.hand(k - 1).start()
                if k < n:
                    self.step(k).start()

            run.append(event)

        def finish():
            for k in range(n):
                self.hand(k).wait_recv()
            self.hand_own().wait_recv()
            for k in range(n):
                self.step(k).wait_send()
                self.hand(k).wait_send()
            self.hand_own().wait_send()

        run.append(finish)
        return run


class Scatter:
    def __init__(self, place, parts, out, order, half, acc, recv, last, sems, local_sem):
        self.place, self.parts, self.out, self.order, self.half = place, parts, out, list(order), half
        self.acc, self.recv, self.last, self.sems, self.local_sem = acc, recv, last, sems, local_sem

    def free(self, k):
        return tuple(b for b in self.place.bits if b not in self.order[: k + 1])

    def step(self, k):
        p, bit = self.place, self.order[k]
        free = self.free(k)
        if k == 0:
            src = self.parts.at[p.index(free, flipped=(bit,))]
        else:
            src = self.acc.at[p.index(free, flipped=(bit,), without=(self.order[0],))]
        return remote(src, self.recv[k], (self.sems.at[0, k], self.sems.at[1, k]), p.partner(bit))

    def local(self):
        p = self.place
        return pltpu.make_async_copy(self.parts.at[p.index(self.free(0))], self.acc, self.local_sem)

    def combine(self, k):
        p, n = self.place, len(self.order)
        free = self.free(k)
        total = 1 << len(free)
        recv = self.recv[k]

        def one(i, carry):
            pos, at, full = 0, [], []
            for bit in free:
                at.append(lax.rem(lax.div(i, 1 << pos), 2))
                pos += 1
            named = dict(zip(free, at))
            full = tuple(named[b] if b in named else p.mine(b) for b in p.bits if b != self.order[0])
            value = self.acc[full].astype(f32) + recv[tuple(at)].astype(f32)
            if k == n - 1:
                self.final(named, value)
            else:
                self.acc[full] = value.astype(self.acc.dtype)
            return carry

        if total == 1:
            one(0, 0)
        else:
            lax.fori_loop(0, total, one, 0)

    def final(self, named, value):
        if self.half is None:
            self.out[...] = value
        else:
            self.last[0, named[SEQ]] = value.astype(bf)

    def trade(self):
        p, n = self.place, len(self.order)
        return remote(self.last.at[0, 1 - p.seq], self.last.at[1, 0], (self.sems.at[0, n], self.sems.at[1, n]), p.partner(SEQ))

    def events(self):
        n = len(self.order)
        run = []

        def begin():
            self.step(0).start()
            self.local().start()

        run.append(begin)
        for k in range(n):

            def event(k=k):
                if k == 0:
                    self.local().wait()
                self.step(k).wait_recv()
                self.combine(k)
                if k + 1 < n:
                    self.step(k + 1).start()
                elif self.half is not None:
                    self.trade().start()

            run.append(event)

        def finish():
            for k in range(n):
                self.step(k).wait_send()
            if self.half is not None:
                self.trade().wait()
                s = self.place.seq
                own, other = self.last[0, s].astype(f32), self.last[1, 0].astype(f32)

                @pl.when(s == 0)
                def _():
                    self.out[:, : self.half] = own
                    self.out[:, self.half :] = other

                @pl.when(s == 1)
                def _():
                    self.out[:, : self.half] = other
                    self.out[:, self.half :] = own

        run.append(finish)
        return run


def orders(count):
    high = list(reversed(range(2, count)))
    return ([*high, 1, SEQ], [*high, SEQ, 1], [1, SEQ, *high])


def run_round_robin(programs):
    most = max(len(p) for p in programs)
    for i in range(most):
        for p in programs:
            if i < len(p):
                p[i]()


def gather_all(clips, full, halves, rows):
    count = clips.bit_length() - 1
    nbits = count + 1
    nf, nh = len(full), len(halves)

    def kernel(*refs):
        ins, outs = refs[: nf + nh + 1], refs[nf + nh + 1 : 2 * (nf + nh + 1)]
        sems, local_sems, row_sems = refs[2 * (nf + nh + 1) :]
        place = Place(clips)
        place.greet()
        row_out = outs[-1]
        give = remote(ins[-1], row_out.at[place.seq], (row_sems.at[0], row_sems.at[1]), place.partner(SEQ))
        give.start()
        keep = pltpu.make_async_copy(ins[-1], row_out.at[place.seq], row_sems.at[2])
        keep.start()
        abc = orders(count)
        programs = []
        for j in range(nh):
            order = [b for b in abc[(0, 2, 2)[j % 3]] if b != SEQ]
            programs.append(Gather(place, ins[nf + j], outs[nf + j], order, halves[j].shape[1] // 2, sems.at[nf + j], local_sems.at[nf + j]).events())
        for j in range(nf):
            programs.append(Gather(place, ins[j], outs[j], abc[j % 3], None, sems.at[j], local_sems.at[j]).events())
        run_round_robin(programs)
        keep.wait()
        give.wait()

    two = (2,) * nbits
    any_spec = pl.BlockSpec(memory_space=pl.ANY)
    vmem = pl.BlockSpec(memory_space=pltpu.VMEM)
    out = pl.pallas_call(
        kernel,
        out_shape=tuple(jax.ShapeDtypeStruct(two + a.shape, a.dtype) for a in full)
        + tuple(jax.ShapeDtypeStruct(two + (a.shape[0], a.shape[1] // 2), a.dtype) for a in halves)
        + (jax.ShapeDtypeStruct((2,) + rows.shape, rows.dtype),),
        in_specs=[vmem] * (nf + nh + 1),
        out_specs=(any_spec,) * (nf + nh + 1),
        scratch_shapes=[
            pltpu.SemaphoreType.DMA((nf + nh, 2, 2 * nbits + 2)),
            pltpu.SemaphoreType.DMA((nf + nh,)),
            pltpu.SemaphoreType.DMA((3,)),
        ],
        compiler_params=pltpu.CompilerParams(collective_id=0, has_side_effects=True),
    )(*full, *halves, rows)
    whole = [o.reshape((-1, a.shape[1])) for o, a in zip(out[:nf], full)]
    half = [o.reshape((-1, a.shape[1] // 2)) for o, a in zip(out[nf : nf + nh], halves)]
    return whole, half, out[-1].reshape((-1, rows.shape[1]))


def scatter_all(clips, full, halves, rows):
    count = clips.bit_length() - 1
    nbits = count + 1
    devices = 2 * clips
    nf, nh = len(full), len(halves)
    two = (2,) * nbits
    parts = [a.reshape(two + (a.shape[0] // devices, a.shape[1])) for a in (*full, *halves)]
    rows = rows.reshape((2, rows.shape[0] // 2, rows.shape[1]))
    abc = [[0, *reversed(o)] for o in orders(count)]

    def order_of(j):
        if j < nf:
            return abc[j % 3]
        return [b for b in abc[(0, 2, 2)[(j - nf) % 3]] if b != SEQ]

    scratch = []
    for j, a in enumerate(parts):
        shard = a.shape[nbits:]
        scratch.append(pltpu.VMEM(two[:-1] + shard, a.dtype))
        for k in range(len(order_of(j))):
            scratch.append(pltpu.VMEM(two[: nbits - 1 - k] + shard, a.dtype))
        scratch.append(pltpu.VMEM((2, 2) + shard, bf) if j >= nf else pltpu.VMEM((8, 128), f32))

    def kernel(*refs):
        n = nf + nh
        ins, outs = refs[: n + 1], refs[n + 1 : 2 * n + 2]
        bufs, (sems, local_sems, row_sems) = list(refs[2 * n + 2 : -3]), refs[-3:]
        place = Place(clips)
        place.greet()
        give = remote(ins[-1].at[1 - place.seq], outs[-1], (row_sems.at[0], row_sems.at[1]), place.partner(SEQ))
        give.start()
        programs = []
        for j in range(n):
            order = order_of(j)
            acc = bufs.pop(0)
            recv = [bufs.pop(0) for _ in order]
            last = bufs.pop(0)
            half = None if j < nf else parts[j].shape[-1]
            programs.append(Scatter(place, ins[j], outs[j], order, half, acc, recv, last, sems.at[j], local_sems.at[j]).events())
        run_round_robin(programs)
        give.wait()

    any_spec = pl.BlockSpec(memory_space=pl.ANY)
    vmem = pl.BlockSpec(memory_space=pltpu.VMEM)
    out = pl.pallas_call(
        kernel,
        out_shape=tuple(
            jax.ShapeDtypeStruct((a.shape[-2], a.shape[-1] * (2 if j >= nf else 1)), f32) for j, a in enumerate(parts)
        )
        + (jax.ShapeDtypeStruct(rows.shape[1:], rows.dtype),),
        in_specs=[any_spec] * (nf + nh + 1),
        out_specs=(vmem,) * (nf + nh) + (any_spec,),
        scratch_shapes=scratch
        + [
            pltpu.SemaphoreType.DMA((nf + nh, 2, nbits + 1)),
            pltpu.SemaphoreType.DMA((nf + nh,)),
            pltpu.SemaphoreType.DMA((2,)),
        ],
        compiler_params=pltpu.CompilerParams(collective_id=1, has_side_effects=True, vmem_limit_bytes=60 << 20),
    )(*parts, rows)
    return out[:nf], out[nf : nf + nh], out[-1]


epsilon = 1e-05
root_half = 0.7071067811865476


def pad_rows(x, to):
    return jnp.pad(x, ((0, to - x.shape[0]), (0, 0)))


def norm_parts(rows_in):
    center = rows_in - jnp.mean(rows_in, axis=-1, keepdims=True)
    scale = lax.rsqrt(jnp.mean(center * center, axis=-1, keepdims=True) + epsilon)
    return center * scale, scale


def norm_back(gy, gain, xhat, scale):
    gt = gy * gain
    return scale * (gt - jnp.mean(gt, axis=-1, keepdims=True) - xhat * jnp.mean(gt * xhat, axis=-1, keepdims=True))


def per_device(
    clips,
    frames,
    norm1_gain,
    norm1_shift,
    query_weight,
    query_bias,
    key_weight,
    value_weight,
    value_bias,
    out_weight,
    out_bias,
    norm2_gain,
    norm2_shift,
    hidden_weight,
    hidden_bias,
    output_weight,
    output_bias,
    out_grad,
):
    seq = lax.axis_index("seq")
    valid, width = frames.shape[1], frames.shape[2]
    half = -(-valid // 256) * 256
    cols = width // 2
    devices = 2 * clips
    vectors = (norm1_gain, norm1_shift, query_bias, value_bias, out_bias, norm2_gain, norm2_shift, hidden_bias, output_bias)
    sizes = [v.shape[0] for v in vectors]
    packed = jnp.pad(jnp.concatenate(vectors), (0, 1024 - sum(sizes))).reshape(8, 128)
    own = pad_rows(frames[0], half)
    (w_hidden, w_output, w_out, small), (w_query, w_key, w_value), both = gather_all(
        clips, [hidden_weight, output_weight, out_weight, packed], [query_weight, key_weight, value_weight], own
    )
    small = small.reshape(devices, 1024).astype(f32)
    unpacked, at = [], 0
    for size in sizes:
        unpacked.append(small[:, at : at + size].reshape(-1))
        at += size
    gain_one, shift_one, b_query, b_value, b_out, gain_two, shift_two, b_hidden, b_output = unpacked
    b_query = lax.dynamic_slice_in_dim(b_query, seq * cols, cols)
    b_value = lax.dynamic_slice_in_dim(b_value, seq * cols, cols)

    xhat_both, scale_both = norm_parts(both.astype(f32))
    normed = (xhat_both * gain_one + shift_one).astype(bf)
    query = (nn(normed, w_query) + b_query).astype(bf)
    key = nn(normed, w_key).astype(bf)
    value = (nn(normed, w_value) + b_value).astype(bf)
    attended_cols, wide_cols, log_cols = attn_fwd(query, key, value, half, valid)

    def trade(x):
        mine = lax.dynamic_slice_in_dim(x, seq * half, half)
        give = lax.dynamic_slice_in_dim(x, (1 - seq) * half, half)
        got = lax.ppermute(give, "seq", [(0, 1), (1, 0)])
        return jnp.where(seq == 0, jnp.concatenate([mine, got], 1), jnp.concatenate([got, mine], 1))

    def trade_back(x):
        mine = lax.dynamic_slice_in_dim(x, seq * cols, cols, 1)
        give = lax.dynamic_slice_in_dim(x, (1 - seq) * cols, cols, 1)
        got = lax.ppermute(give, "seq", [(0, 1), (1, 0)])
        return jnp.where(seq == 0, jnp.concatenate([mine, got], 0), jnp.concatenate([got, mine], 0))

    attended = trade(attended_cols)
    hidden_in = own.astype(f32) + nn(attended, w_out) + b_out
    xhat_two, scale_two = norm_parts(hidden_in)
    normed_two = (xhat_two * gain_two + shift_two).astype(bf)
    pre_act = nn(normed_two, w_hidden) + b_hidden
    cdf = 0.5 * (1.0 + lax.erf(pre_act * root_half))
    acted = (pre_act * cdf).astype(bf)
    encoded = (hidden_in + nn(acted, w_output) + b_output).astype(bf)[:valid]

    grad_ff = pad_rows(out_grad[0], half)
    grad_out = grad_ff.astype(f32)
    grad_w_output = tn(acted, grad_ff)
    slope = cdf + pre_act * jnp.exp(-0.5 * pre_act * pre_act) * 0.3989422804014327
    grad_pre = (nt(grad_ff, w_output) * slope).astype(bf)
    grad_w_hidden = tn(normed_two, grad_pre)
    gy_two = nt(grad_pre, w_hidden)
    grad_hidden_in = grad_out + norm_back(gy_two, gain_two, xhat_two, scale_two)
    grad_branch = grad_hidden_in.astype(bf)
    grad_w_out = tn(attended, grad_branch)
    grad_attended = nt(grad_branch, w_out).astype(bf)

    query_grad, key_grad, value_grad = attn_bwd(
        query, key, value, trade_back(grad_attended), wide_cols, log_cols, half, valid
    )
    grad_w_query = tn(normed, query_grad)
    grad_w_key = tn(normed, key_grad)
    grad_w_value = tn(normed, value_grad)
    gy_one = nt(query_grad, w_query) + nt(key_grad, w_key) + nt(value_grad, w_value)

    def sums(x):
        return jnp.sum(x.astype(f32), axis=0)

    def spread(x):
        return lax.dynamic_update_slice_in_dim(jnp.zeros((width,), f32), x, seq * cols, 0)

    vector_sums = (
        sums(gy_one * xhat_both),
        sums(gy_one),
        spread(sums(query_grad)),
        spread(sums(value_grad)),
        sums(grad_branch),
        sums(gy_two * xhat_two),
        sums(gy_two),
        sums(grad_pre),
        sums(grad_ff),
    )
    packed_sums = jnp.concatenate([v.reshape(devices, -1) for v in vector_sums], axis=1)
    packed_sums = jnp.pad(packed_sums, ((0, 0), (0, 1024 - packed_sums.shape[1]))).reshape(devices * 8, 128)
    (own_hidden, own_output, own_out, own_small), (own_query, own_key, own_value), gy_got = scatter_all(
        clips,
        [grad_w_hidden.astype(bf), grad_w_output.astype(bf), grad_w_out.astype(bf), packed_sums],
        [grad_w_query.astype(bf), grad_w_key.astype(bf), grad_w_value.astype(bf)],
        gy_one.astype(bf),
    )
    gy_mine = lax.dynamic_slice_in_dim(gy_one, seq * half, half) + gy_got.astype(f32)
    xhat_one, scale_one = norm_parts(own.astype(f32))
    frames_grad = (grad_hidden_in + norm_back(gy_mine, gain_one, xhat_one, scale_one)).astype(bf)[:valid]

    own_small = own_small.reshape(-1)
    owned, at = [], 0
    for size in sizes:
        owned.append(own_small[at : at + size])
        at += size
    return (
        encoded[None],
        frames_grad[None],
        owned[0],
        owned[1],
        own_query,
        owned[2],
        own_key,
        own_value,
        owned[3],
        own_out,
        owned[4],
        owned[5],
        owned[6],
        own_hidden,
        owned[7],
        own_output,
        owned[8],
    )


def solution(mesh):
    rows, vector, matrix = P("clip", "seq", None), P(("clip", "seq")), P(("clip", "seq"), None)
    placed = (
        rows,
        vector,
        vector,
        matrix,
        vector,
        matrix,
        matrix,
        vector,
        matrix,
        vector,
        vector,
        vector,
        matrix,
        vector,
        matrix,
        vector,
        rows,
    )
    weights = placed[1:-1]
    return jax.shard_map(
        functools.partial(per_device, mesh.shape["clip"]),
        mesh=mesh,
        in_specs=placed,
        out_specs=(rows, rows) + weights,
        check_vma=False,
    )
```

time: 1460 us -> 419 us (0.29)
  waiting for transfers between devices: 947 us -> 8.55 us
  Pallas kernels: 0 us -> 275 us
  matrix products: 258 us -> 73 us
  blocking collectives: 83.2 us -> 0 us
  other arithmetic: 86 us -> 18.9 us
  local copies, waits for them, and re-layouts: 58 us -> 34.3 us
    reduce_scatter x6 -> x0, waiting for transfers between devices: 603 us -> none  [the longest x1 142 us: per_device(): lax.psum_scatter(grad_w_hidden, ('clip', 'seq'), scatter_dimension=0, til...]
    pallas_call x0 -> x4, Pallas kernels: none -> 275 us  [the longest x1 97.7 us: gather_all(): pl.pallas_call(kernel, out_shape=tuple((jax.ShapeDtypeStruct(two + a.shap...]
    all_gather x8 -> x0, waiting for transfers between devices: 233 us -> none  [the longest x1 54.2 us: per_device(): lax.all_gather(output_weight, ('clip', 'seq'), axis=0, tiled=True)]
    dot_general x39 -> x18, matrix products: 258 us -> 73 us  [the longest x6 25.3 us: nt(): lax.dot_general(a, b, (((1,), (1,)), ((), ())), preferred_element_type=f32)]
    unnamed x16 -> x0, waiting for transfers between devices: 111 us -> none
    unnamed x2 -> x0, blocking collectives: 83.2 us -> none
    convert_element_type x12 -> x1, other arithmetic: 40.5 us -> 1.53 us  [per_device(): normed = (xhat_both * gain_one + shift_one).astype(bf)]
    reduce_sum x12 -> x9, other arithmetic: 41.5 us -> 9.31 us  [the longest x1 3.19 us: norm_back(): jnp.mean(gt, axis=-1, keepdims=True)]
  transfers between devices with their start and end apart: 15 -> 2, of which waited for: 14 -> 2; matrix products, arithmetic and copies ran while one was open for 14% -> 5% of each run, Pallas kernels for 0% -> 0%
where the time goes in v1:
time: 419 us; the launch traced here: 415 us
  Pallas kernels  275 us (66%)
  matrix products  73 us (17%)
  local copies, waits for them, and re-layouts  34.3 us (8%)
  other arithmetic  18.9 us (5%)
  waiting for transfers between devices  8.55 us (2%)
    pallas_call x1, Pallas kernels, gather_all(): pl.pallas_call(kernel, out_shape=tuple((jax.ShapeDtypeStruct(two + a.shap...  97.7 us
    pallas_call x1, Pallas kernels, scatter_all(): pl.pallas_call(kernel, out_shape=tuple((jax.ShapeDtypeStruct((a.shape[-2]...  94.8 us
    pallas_call x1, Pallas kernels, attn_bwd(): pl.pallas_call(functools.partial(bwd_kernel, half, valid, tq), grid=(np_,...  48.7 us
    pallas_call x1, Pallas kernels, attn_fwd(): pl.pallas_call(functools.partial(fwd_kernel, half, valid, tq), grid=(np_,...  34.3 us
    dot_general x6, matrix products, nt(): lax.dot_general(a, b, (((1,), (1,)), ((), ())), preferred_element_type=f32)  25.3 us
    dot_general x6, matrix products, nn(): lax.dot_general(a, b, (((1,), (0,)), ((), ())), preferred_element_type=f32)  25.2 us
    dot_general x6, matrix products, tn(): lax.dot_general(a, b, (((0,), (0,)), ((), ())), preferred_element_type=f32)  22.5 us
  transfers between devices with their start and end apart: 2, of which 2 were waited for; matrix products, arithmetic and copies ran while one was open for 5% of the time, Pallas kernels for 0%

profile of v1, /device:TPU:0, one launch (start us, length us, event | category | flops | bytes accessed | tf_op | source)
XLA Modules:
  0.0 415.0 jit_solution(6781472696525993665)
XLA Ops:
  0.7 6.1 %concatenate.18 = bf16[288]{0:T(512)(128)(2,1)S(1)} concatenate(bf16[24]{0:T(256)(128)(2,1)} %param.18, bf16[24]{0:T(256)(128)(2,1)} %param.19, bf16[24]{0:T(256)(128)(2,1)} %param.21, bf16[24]{0:T(256)(128)(2,1)} %param.24, bf16[24]{0:T(256)(128)(2,1)} %param.26, bf16[24]{0:T(256)(128)(2,1)} %param.27, bf16[24]{0:T(256)(128)(2,1)} %param.28, bf16[96]{0:T(256)(128)(2,1)} %param.30, ...), dimensions={0} | concatenate | bytes 1152 | tf_op jit(solution)/shard_map/concatenate | solution.py:542
  7.4 2.4 pad.15.refs_7_
  9.7 97.7 %shard_map.296 = (bf16[2,2,2,2,2,24,3072]{6,5,4,3,2,1,0:T(8,128)(2,1)}, bf16[2,2,2,2,2,96,768]{6,5,4,3,2,1,0:T(8,128)(2,1)}, bf16[2,2,2,2,2,24,768]{6,5,4,3,2,1,...) custom-call(bf16[24,3072]{1,0:T(8,128)(2,1)} %refs_0_.1, ...), custom_call_target="tpu_custom_call" | custom-call | tf_op jit(solution)/shard_map/pallas_call | solution.py:414
  107.4 2.2 convert_reduce_fusion.1
  113.5 2.4 convolution_convert_fusion.2.k_ref
  116.0 2.5 fusion.10.v_ref
  118.5 2.4 fusion.9.q_ref
  120.9 34.3 %shard_map.297 = (bf16[1536,384]{1,0:T(8,128)(2,1)}, f32[1536,384]{1,0:T(8,128)}, bf16[6,1536,128]{2,1,0:T(8,128)(2,1)}) custom-call(bf16[1536,384]{1,0:T(8,128)(2,1)} %fusion.9.q_ref, bf16[1536,384]{1,0:T(8,128)(2,1)} %convolution_convert_fusion.2.k_ref, bf16[1536,384]{1,0:T(8,128)(2,1)} %fusion.10.v_ref), custom_call_target="tpu_custom_call" | custom-call | tf_op jit(solution)/shard_map/pallas_call | solution.py:65
  155.2 2.4 constant_dynamic-slice_fusion.3
  167.5 6.0 %collective-permute-done = bf16[768,384]{1,0:T(8,128)(2,1)} collective-permute-done((bf16[768,384]{1,0:T(8,128)(2,1)}, bf16[768,384]{1,0:T(8,128)(2,1)}, u32[]{:S(2)}, u32[]{:S(2)}) %collective-permute-start) | collective-permute-done | bytes 589856 | tf_op jit(solution)/shard_map/ppermute | solution.py:566
  173.5 3.3 fusion.33
  177.6 9.3 %multiply_convert_fusion = (bf16[768,3072]{1,0:T(8,128)(2,1)}, f32[768,3072]{1,0:T(8,128)}) fusion(f32[3072]{0:T(1024)S(1)} %add.177, bf16[768,3072]{1,0:T(8,128)(2,1)S(1)} %bitcast.111, f32[768,768]{1,0:T(8,128)S(1)} %get-tuple-element.97, f32[768]{0:T(1024)S(1)} %copy-done.42, f32[768]{0:T(1024)S(1)} %mul.187, f32[768]{0:T(1024)S(1)} %add_rsqrt_fusion.2, ...), kind=kOutput, calls=%fused_computation.8 | convolution fusion | flops 3640983552 | bytes 21258240 | tf_op jit(solution)/shard_map/dot_general | solution.py:16
  186.9 9.7 %convert_reduce_fusion = (f32[3072]{0:T(1024)}, bf16[768,3072]{1,0:T(8,128)(2,1)S(1)}) fusion(f32[768,3072]{1,0:T(8,128)} %get-tuple-element.99, f32[3072]{0:T(1024)S(1)} %add.177, bf16[3072,768]{1,0:T(8,128)(2,1)S(1)} %bitcast.107, bf16[750,768]{1,0:T(8,128)(2,1)S(1)} %bitcast.84), kind=kOutput, calls=%fused_computation.7 | convolution fusion | flops 3654546432 | bytes 20050944 | tf_op jit(solution)/shard_map/dot_general | solution.py:14
  196.6 5.0 %multiply_reduce_fusion.3 = (f32[768]{0:T(1024)}, f32[768]{0:T(1024)S(1)}, f32[768]{0:T(1024)S(1)}, f32[768]{0:T(1024)}, f32[768,768]{1,0:T(8,128)S(1)}) fusion(f32[768,768]{1,0:T(8,128)S(1)} %get-tuple-element.97, f32[768]{0:T(1024)S(1)} %add_rsqrt_fusion.2, f32[768]{0:T(1024)S(1)} %broadcast_multiply_fusion.6, f32[768]{0:T(1024)S(1)} %mul.187, ...), kind=kOutput, calls=%fused_computation.36 | convolution fusion | flops 3629184000 | bytes 14177280 | tf_op jit(solution)/shard_map/dot_general | solution.py:14
  201.5 6.5 %convolution_convert_fusion.1 = bf16[768,3072]{1,0:T(8,128)(2,1)} fusion(bf16[768,3072]{1,0:T(8,128)(2,1)S(1)} %get-tuple-element.103, f32[768,768]{1,0:T(8,128)S(1)} %get-tuple-element.97, f32[768]{0:T(1024)S(1)} %copy-done.42, f32[768]{0:T(1024)S(1)} %mul.187, f32[768]{0:T(1024)S(1)} %add_rsqrt_fusion.2, f32[768]{0:T(1024)S(1)} %broadcast_multiply_fusion.6), kind=kOutput, calls=%fused_computation.11 | convolution fusion | flops 3629187072 | bytes 11808768 | tf_op jit(solution)/shard_map/dot_general | solution.py:18
  208.0 5.8 %convolution_convert_fusion = bf16[3072,768]{1,0:T(8,128)(2,1)} fusion(bf16[768,3072]{1,0:T(8,128)(2,1)S(1)} %copy-done.46, bf16[750,768]{1,0:T(8,128)(2,1)S(1)} %bitcast.85), kind=kOutput, calls=%fused_computation.10 | convolution fusion | flops 3626237952 | bytes 10589184 | tf_op jit(solution)/shard_map/dot_general | solution.py:18
  213.8 5.2 %fusion.34 = f32[768,768]{1,0:T(8,128)} fusion(bf16[768,3072]{1,0:T(8,128)(2,1)S(1)} %copy-done.46, bf16[3072,768]{1,0:T(8,128)(2,1)S(1)} %bitcast.108), kind=kOutput, calls=%fused_computation.94 | convolution fusion | flops 3623878656 | bytes 11796480 | tf_op jit(solution)/shard_map/dot_general | solution.py:16
  223.0 1.6 collective-permute-start.1
  228.2 3.8 fusion.18
  232.0 3.5 convolution_convert_fusion.3
  235.5 2.6 collective-permute-done.1
  238.1 2.6 maximum_select_fusion.1.g_ref
  240.7 48.7 %shard_map.298 = (bf16[1536,384]{1,0:T(8,128)(2,1)}, bf16[1536,384]{1,0:T(8,128)(2,1)}, bf16[1536,384]{1,0:T(8,128)(2,1)}) custom-call(bf16[1536,384]{1,0:T(8,128)(2,1)} %fusion.9.q_ref, bf16[1536,384]{1,0:T(8,128)(2,1)} %convolution_convert_fusion.2.k_ref, bf16[1536,384]{1,0:T(8,128)(2,1)} %fusion.10.v_ref, bf16[1536,384]{1,0:T(8,128)(2,1)} %maximum_select_fusion.1.g_ref, ...), custom_call_target="tpu_custom_call" | custom-call | tf_op jit(solution)/shard_map/pallas_call | solution.py:123
  289.5 2.8 fusion.36
  293.8 5.3 %fusion.29 = (f32[768]{0:T(1024)}, f32[768]{0:T(1024)}, bf16[1536,768]{1,0:T(8,128)(2,1)}, bf16[1536,768]{1,0:T(8,128)(2,1)S(1)}, f32[1536,768]{1,0:T(8,128)}) fusion(f32[1536]{0:T(1024)S(1)} %copy-done.37, f32[1536]{0:T(1024)S(1)} %copy-done.38, bf16[2,768,768]{2,1,0:T(8,128)(2,1)S(1)} %copy-done, f32[768]{0:T(1024)S(1)} %copy-done.36, ...), kind=kOutput, calls=%fused_computation.89 | convolution fusion | flops 920123904 | bytes 23027712 | tf_op jit(solution)/shard_map/dot_general | solution.py:14
  299.1 2.2 convolution_convert_fusion.5
  301.4 2.2 convolution_convert_fusion.6
  303.6 2.2 convolution_convert_fusion.7
  308.2 94.8 %shard_map.299 = (f32[24,3072]{1,0:T(8,128)}, f32[96,768]{1,0:T(8,128)}, f32[24,768]{1,0:T(8,128)}, f32[8,128]{1,0:T(8,128)}, f32[24,768]{1,0:T(8,128)}, /*index...) custom-call(bf16[2,2,2,2,2,24,3072]{6,5,4,3,2,1,0:T(8,128)(2,1)} %bitcast.78, ...), custom_call_target="tpu_custom_call" | custom-call | tf_op jit(solution)/shard_map/pallas_call | solution.py:477
  403.1 1.6 fusion.32
  405.9 3.2 fusion.30
  409.2 1.6 fusion.19
  (165 shorter events, 31.5 us)
Async XLA Ops:
  107.4 2.4 copy-start
  107.4 3.3 copy-start.25
  110.7 2.8 copy-start.32
  110.7 2.8 copy-start.11
  113.5 2.4 copy-start.12
  116.0 2.5 copy-start.14
  120.9 41.6 %copy-start.2 = (bf16[1,750,768]{2,1,0:T(8,128)(2,1)S(1)}, bf16[1,750,768]{2,1,0:T(8,128)(2,1)}, u32[]{:S(2)}) copy-start(bf16[1,750,768]{2,1,0:T(8,128)(2,1)} %param.17) | copy-start | bytes 3456004
  157.5 15.9 %collective-permute-start = (bf16[768,384]{1,0:T(8,128)(2,1)}, bf16[768,384]{1,0:T(8,128)(2,1)}, u32[]{:S(2)}, u32[]{:S(2)}) collective-permute-start(bf16[768,384]{1,0:T(8,128)(2,1)} %get-tuple-element.77), channel_id=1, source_target_pairs={{0,1},{1,0},{2,3},{3,2},{4,5},{5,4},{6,7},{7,6},{8,9},{9,8},{10,11... | collective-permute-start | bytes 1769480 | tf_op jit(solution)/shard_map/ppermute | solution.py:566
  167.0 6.5 %copy-start.33 = (f32[768]{0:T(1024)}, f32[768]{0:T(1024)S(1)}, u32[]{:S(2)}) copy-start(f32[768]{0:T(1024)S(1)} %broadcast_multiply_fusion.3) | copy-start | bytes 9220
  173.5 3.8 slice-start.2
  173.5 3.8 slice-start.3
  176.8 42.2 %copy-start.1 = (f32[768,768]{1,0:T(8,128)}, f32[768,768]{1,0:T(8,128)S(1)}, u32[]{:S(2)}) copy-start(f32[768,768]{1,0:T(8,128)S(1)} %get-tuple-element.97) | copy-start | bytes 7077892
  176.9 10.0 %slice-start = ((s8[4718592]{0:T(1024)(128)(4,1)}), s8[4194304]{0:T(1024)(128)(4,1)S(1)}, s32[]{:S(2)}) async-start(s8[4718592]{0:T(1024)(128)(4,1)} %bitcast.105), calls=%async_computation | async-start | bytes 8388608
  177.6 9.3 %copy-start.10 = (bf16[1,750,768]{2,1,0:T(8,128)(2,1)S(1)}, bf16[1,750,768]{2,1,0:T(8,128)(2,1)}, u32[]{:S(2)}) copy-start(bf16[1,750,768]{2,1,0:T(8,128)(2,1)} %param.33) | copy-start | bytes 3456004
  177.6 9.3 %slice-start.1 = ((s8[4718592]{0:T(1024)(128)(4,1)}), s8[524288]{0:T(1024)(128)(4,1)S(1)}, s32[]{:S(2)}) async-start(s8[4718592]{0:T(1024)(128)(4,1)} %bitcast.105), calls=%async_computation.1 | async-start | bytes 1048576
  201.5 6.5 %copy-start.46 = (bf16[768,3072]{1,0:T(8,128)(2,1)S(1)}, bf16[768,3072]{1,0:T(8,128)(2,1)}, u32[]{:S(2)}) copy-start(bf16[768,3072]{1,0:T(8,128)(2,1)} %get-tuple-element.98) | copy-start | bytes 14155780
  221.9 3.5 copy-start.44
  221.9 4.2 %copy-start.43 = (f32[768]{0:T(1024)S(1)}, f32[768]{0:T(1024)}, u32[]{:S(2)}) copy-start(f32[768]{0:T(1024)} %get-tuple-element.68) | copy-start | bytes 9220
  221.9 6.3 %copy-start.39 = (f32[768]{0:T(1024)S(1)}, f32[768]{0:T(1024)}, u32[]{:S(2)}) copy-start(f32[768]{0:T(1024)} %add.183) | copy-start | bytes 9220
  223.0 15.1 %collective-permute-start.1 = (bf16[768,384]{1,0:T(8,128)(2,1)}, bf16[768,384]{1,0:T(8,128)(2,1)}, u32[]{:S(2)}, u32[]{:S(2)}) collective-permute-start(bf16[768,384]{1,0:T(8,128)(2,1)} %get-tuple-element.75), channel_id=1, source_target_pairs={{0,1},{1,0},{2,3},{3,2},{4,5},{5,4},{6,7},{7,6},{8,9},{9,8},{10,11... | collective-permute-start | bytes 1769480 | tf_op jit(solution)/shard_map/ppermute | solution.py:572
  228.2 3.8 copy-start.4
  228.2 3.8 copy-start.18
  232.0 6.1 %copy-start.9 = (bf16[768,384]{1,0:T(8,128)(2,1)S(1)}, bf16[768,384]{1,0:T(8,128)(2,1)}, u32[]{:S(2)}) copy-start(bf16[768,384]{1,0:T(8,128)(2,1)} %get-tuple-element.74) | copy-start | bytes 1769476
  240.7 48.7 %copy-start.17 = (bf16[2,2,2,2,2,24,384]{6,5,4,3,2,1,0:T(8,128)(2,1)S(1)}, bf16[2,2,2,2,2,24,384]{6,5,4,3,2,1,0:T(8,128)(2,1)}, u32[]{:S(2)}) copy-start(bf16[2,2,2,2,2,24,384]{6,5,4,3,2,1,0:T(8,128)(2,1)} %get-tuple-element.42) | copy-start | bytes 1769476
  289.4 2.8 copy-start.6
  289.4 2.8 copy-start.15
  308.2 97.7 %copy-start.34 = (f32[768]{0:T(1024)S(1)}, f32[768]{0:T(1024)}, u32[]{:S(2)}) copy-start(f32[768]{0:T(1024)} %copy-done.33) | copy-start | bytes 9220
  405.9 3.2 copy-start.5
  409.2 2.9 copy-start.22
  409.2 3.5 copy-start.21
  409.2 4.1 copy-start.20
  409.2 4.9 %copy-start.19 = (f32[96,768]{1,0:T(8,128)S(1)}, f32[96,768]{1,0:T(8,128)}, u32[]{:S(2)}) copy-start(f32[96,768]{1,0:T(8,128)} %get-tuple-element.138) | copy-start | bytes 884740
  (21 other events, 31.8 us)
